TPU v7x, 32 devices: a whole 2x2x4 slice. The times are simulated.
32 devices in a mesh: dp: 4 (over z), expert: 8 (over y, x, core).
Axes of the slice: x: 2, y: 2, z: 4, core: 2. Of those that a mesh axis runs over, the one named last changes fastest.
Arguments:
- tokens: bfloat16 [512, 7168], P('expert'), may hold values from -6 to 6
- routes: int32 [512, 8], P('expert'), may hold values from 0 to 7, all different within a row; in each aligned block of 64 rows (0 to 63, 64 to 127, ...) at most 64 rows name the same one
- route_weight: int32 [512, 8], P('expert'), may hold values from 1 to 4096
- w_gate: bfloat16 [8, 7168, 2048], P('expert', None, 'dp'), may hold values from -0.0625 to 0.0625
- w_up: bfloat16 [8, 7168, 2048], P('expert', None, 'dp'), may hold values from -0.0625 to 0.0625
- w_down: bfloat16 [8, 2048, 7168], P('expert', 'dp'), may hold values from -0.125 to 0.125
- prev_inputs: bfloat16 [4, 8, 64, 7168], P('dp', 'expert'), may hold values from -6 to 6
Outputs:
- mixed: bfloat16 [512, 7168], P('expert', 'dp')
- hessian: float32 [7168, 8, 128], P('dp', 'expert')
Inputs may be any that keep to these rules, and one draw needn't show every extreme that they name: `routes`: in each aligned block of 64 rows (the rows of one index of expert) no expert is named more than 64 times, a bound that some block reaches; the 8 experts of a token differ.
All inputs are finite; a program needn't handle non-finite values.
Results may differ from a plain program's by a relative error of at most 0.014.
Values may be sent and summed in bfloat16 or wider, within the bound.
A program may use at most 128 MiB of HBM per device.

v0:
```python
import jax
import jax.numpy as jnp
from jax import lax
from jax.sharding import PartitionSpec as P

HESS_COLS = 128


def route_slots(flat_ids, experts_all):
    onehot = (flat_ids[:, None] == jnp.arange(experts_all, dtype=jnp.int32)[None, :]).astype(
        jnp.int32
    )
    earlier = jnp.cumsum(onehot, axis=0) - onehot
    return jnp.sum(earlier * onehot, axis=1)


def combine_rows(back, places, shares, tok_dev, top):
    columns = back.shape[-1]
    rows = back.reshape(-1, columns)[places]
    weighted = rows.astype(jnp.float32) * shares.reshape(-1, 1)
    return jnp.sum(weighted.reshape(tok_dev, top, columns), axis=1)


def shards(tokens, routes, route_weight, w_gate, w_up, w_down, prev_inputs):
    tok_dev, top = routes.shape
    exp_dev = w_gate.shape[0]
    width = tokens.shape[1]
    n_expert = lax.axis_size("expert")
    n_dp = lax.axis_size("dp")
    experts_all = exp_dev * n_expert
    capacity = min(tok_dev, tok_dev * top * 5 // (4 * experts_all))
    flat_ids = routes.reshape(-1)
    slots = route_slots(flat_ids, experts_all)
    places = flat_ids * capacity + slots
    weight_counts = route_weight.astype(jnp.float32)
    shares = 2.5 * weight_counts / jnp.sum(weight_counts, axis=1, keepdims=True)
    picks = jnp.arange(experts_all * capacity, dtype=jnp.int32)[:, None] == places[None, :]
    placing = jnp.any(picks.reshape(experts_all * capacity, tok_dev, top), axis=2).astype(
        jnp.bfloat16
    )
    outgoing = jnp.dot(placing, tokens, preferred_element_type=jnp.float32).astype(jnp.bfloat16)
    outgoing = outgoing.reshape(experts_all, capacity, width)
    arrived = lax.all_to_all(outgoing, "expert", split_axis=0, concat_axis=0, tiled=True)
    arrived = arrived.reshape(n_expert, exp_dev, capacity, width)
    gate = jnp.einsum("sjcd,jdf->sjcf", arrived, w_gate, preferred_element_type=jnp.float32)
    up = jnp.einsum("sjcd,jdf->sjcf", arrived, w_up, preferred_element_type=jnp.float32)
    history = prev_inputs.reshape(prev_inputs.shape[1], prev_inputs.shape[2], width)
    head_cols = history[:, :, :HESS_COLS]
    gram_scale = 2.0 / (n_dp * history.shape[1])
    hessian = lax.psum_scatter(
        (
            jnp.einsum("jrd,jrh->djh", history, head_cols, preferred_element_type=jnp.float32)
            * gram_scale
        ).astype(jnp.bfloat16),
        "dp",
        scatter_dimension=0,
        tiled=True,
    ).astype(jnp.float32)
    hidden = (jax.nn.silu(gate) * up).astype(jnp.bfloat16)
    partial_out = jnp.einsum("sjcf,jfd->sjcd", hidden, w_down, preferred_element_type=jnp.float32)
    partial_out = partial_out.astype(jnp.bfloat16)
    back = lax.all_to_all(
        partial_out.reshape(experts_all, capacity, width),
        "expert",
        split_axis=0,
        concat_axis=0,
        tiled=True,
    )
    own_sum = combine_rows(back, places, shares, tok_dev, top)
    mixed = lax.psum_scatter(own_sum.astype(jnp.bfloat16), "dp", scatter_dimension=1, tiled=True)
    return (mixed, hessian)


def solution(mesh):
    placed = (
        P("expert", None),
        P("expert", None),
        P("expert", None),
        P("expert", None, "dp"),
        P("expert", None, "dp"),
        P("expert", "dp", None),
        P("dp", "expert", None, None),
    )
    return jax.shard_map(
        shards,
        mesh=mesh,
        in_specs=placed,
        out_specs=(P("expert", "dp"), P("dp", "expert", None)),
        check_vma=False,
    )
```

profile of v0, /device:TPU:0, one launch (start us, length us, event | category | flops | bytes accessed | tf_op | source)
XLA Modules:
  0.0 264.7 jit_solution(14011733482339253302)
XLA Ops:
  7.2 0.0 copy-start
  7.2 0.9 copy.17
  8.0 0.1 eq.44
  8.1 0.1 eq.40
  8.2 1.1 reduce-window.6
  9.4 0.2 slice_reduce_fusion
  9.6 0.1 fusion.26
  9.7 0.1 reduce_sum.32
  9.8 0.4 fusion.23
  10.2 0.0 copy-done
  10.2 0.0 slice-start
  10.2 2.1 convolution_convert_fusion.1
  12.4 0.0 slice-start.1
  12.4 0.0 slice-start.2
  12.4 88.0 %all_to_all.10 = bf16[8,64,7168]{2,1,0:T(8,128)(2,1)S(1)} all-to-all(bf16[8,64,7168]{2,1,0:T(8,128)(2,1)S(1)} %bitcast.73), channel_id=1, replica_groups=mesh['dp'=4,'expert'=8] {'expert'}, dimensions={0} | all-to-all | bytes 14680064 | tf_op jit(solution)/shard_map/all_to_all | solution.py:43
  100.4 0.0 slice-done
  100.4 0.0 slice-done.1
  100.4 0.0 slice-start.3
  100.4 3.9 %fusion.8 = f32[8,1,64,512]{3,2,0,1:T(8,128)S(1)} fusion(bf16[8,64,7168]{2,1,0:T(8,128)(2,1)S(1)} %all_to_all.10, bf16[1,7168,512]{2,1,0:T(8,128)(2,1)S(1)} %bitcast.78), kind=kOutput, calls=%fused_computation.13 | convolution fusion | flops 3758096384 | bytes 15728640 | tf_op jit(solution)/shard_map/sjcd,jdf->sjcf/dot_general | solution.py:45
  104.3 0.0 slice-done.2
  104.4 0.0 slice-done.3
  104.4 4.0 %fusion.20 = bf16[8,64,512]{2,1,0:T(8,128)(2,1)S(1)} fusion(bf16[8,64,7168]{2,1,0:T(8,128)(2,1)S(1)} %all_to_all.10, bf16[1,7168,512]{2,1,0:T(8,128)(2,1)S(1)} %bitcast.80, f32[8,1,64,512]{3,2,0,1:T(8,128)S(1)} %fusion.8), kind=kOutput, calls=%fused_computation.17 | convolution fusion | flops 3759669248 | bytes 16252928 | tf_op jit(solution)/shard_map/sjcd,jdf->sjcf/dot_general | solution.py:46
  108.4 9.1 %convolution_convert_fusion = bf16[8,64,7168]{2,1,0:T(8,128)(2,1)} fusion(bf16[8,64,512]{2,1,0:T(8,128)(2,1)S(1)} %fusion.20, bf16[1,512,7168]{2,1,0:T(8,128)(2,1)} %param.12), kind=kOutput, calls=%fused_computation.3 | convolution fusion | flops 3761766400 | bytes 15204352 | tf_op jit(solution)/shard_map/sjcf,jfd->sjcd/dot_general | solution.py:60
  117.5 0.0 copy-start.1
  117.5 0.0 copy-start.2
  117.5 5.0 %all-to-all-start.1 = ((bf16[8,64,7168]{2,1,0:T(8,128)(2,1)}), bf16[8,64,7168]{2,1,0:T(8,128)(2,1)}, u32[]{:S(2)}, u32[]{:S(2)}) async-start(bf16[8,64,7168]{2,1,0:T(8,128)(2,1)} %convolution_convert_fusion), calls=%async_computation.1 | async-start | bytes 14680064 | tf_op jit(solution)/shard_map/all_to_all | solution.py:62
  122.5 0.0 reduce-scatter.5.cloned.1.call-start
  122.5 0.0 copy-done.1
  122.6 1.9 fusion.2
  124.5 0.0 reduce-scatter.5.cloned.1.call-update
  124.5 0.2 reduce-scatter.3.cloned.1.call-start
  124.7 0.1 mul.58
  124.8 0.0 copy-done.2
  124.8 0.1 copy.20
  125.0 80.3 %all-to-all-done.1 = bf16[8,64,7168]{2,1,0:T(8,128)(2,1)} async-done(((bf16[8,64,7168]{2,1,0:T(8,128)(2,1)}), bf16[8,64,7168]{2,1,0:T(8,128)(2,1)}, u32[]{:S(2)}, u32[]{:S(2)}) %all-to-all-start.1) | async-done | bytes 7340064 | tf_op jit(solution)/shard_map/all_to_all | solution.py:62
  205.3 17.9 %gather_fusion = bf16[512,7168]{1,0:T(8,128)(2,1)} fusion(bf16[512,7168]{1,0:T(8,128)(2,1)} %bitcast.18, s32[1024]{0:T(1024)S(1)} %pad_clamp_fusion), kind=kCustom, calls=%fused_computation | custom fusion | bytes 14682112 | tf_op jit(solution)/shard_map/gather | solution.py:19
  223.2 9.8 %fusion = bf16[64,7168]{1,0:T(8,128)(2,1)} fusion(bf16[512,7168]{1,0:T(8,128)(2,1)} %gather_fusion, f32[64,8]{1,0:T(8,128)S(1)} %copy.20), kind=kLoop, calls=%fused_computation.2 | loop fusion | flops 10551296 | bytes 8259584 | tf_op jit(solution)/shard_map/reduce_sum | solution.py:21
  233.1 0.0 reduce-scatter.3.cloned.1.call-update
  233.1 0.0 reduce-scatter.5.cloned.1.call-done
  233.1 3.0 %copy.21 = f32[1792,1,128]{2,1,0:T(1,128)} copy(bf16[1792,1,128]{0,2,1:T(8,128)(2,1)} %reduce-scatter.5.cloned.1.call-done) | data formatting | bytes 1376256
  236.1 21.8 %reduce-scatter.3.cloned.1.call-done = bf16[64,1792]{1,0:T(8,128)(2,1)} async-done(((bf16[64,7168]{1,0:T(8,128)(2,1)}), bf16[64,1792]{1,0:T(8,128)(2,1)}) %reduce-scatter.3.cloned.1.call-update) | async-done | bytes 229392 | tf_op jit(solution)/shard_map/reduce_scatter | solution.py:70
  (10 shorter events, 0.1 us)
Async XLA Ops:
  7.2 3.1 %copy-start = (bf16[64,7168]{1,0:T(8,128)(2,1)S(1)}, bf16[64,7168]{1,0:T(8,128)(2,1)}, u32[]{:S(2)}) copy-start(bf16[64,7168]{1,0:T(8,128)(2,1)} %param.7) | copy-start | bytes 2752516
  10.2 90.2 %slice-start = ((s8[7340032]{0:T(1024)(128)(4,1)}), s8[4194304]{0:T(1024)(128)(4,1)S(1)}, s32[]{:S(2)}) async-start(s8[7340032]{0:T(1024)(128)(4,1)} %bitcast.77), calls=%async_computation.6 | async-start | bytes 8388608
  12.4 88.0 %slice-start.1 = ((s8[7340032]{0:T(1024)(128)(4,1)}), s8[3145728]{0:T(1024)(128)(4,1)S(1)}, s32[]{:S(2)}) async-start(s8[7340032]{0:T(1024)(128)(4,1)} %bitcast.77), calls=%async_computation.7 | async-start | bytes 6291456
  12.4 92.0 %slice-start.2 = ((s8[7340032]{0:T(1024)(128)(4,1)}), s8[4194304]{0:T(1024)(128)(4,1)S(1)}, s32[]{:S(2)}) async-start(s8[7340032]{0:T(1024)(128)(4,1)} %bitcast.79), calls=%async_computation.8 | async-start | bytes 8388608
  100.4 4.0 %slice-start.3 = ((s8[7340032]{0:T(1024)(128)(4,1)}), s8[3145728]{0:T(1024)(128)(4,1)S(1)}, s32[]{:S(2)}) async-start(s8[7340032]{0:T(1024)(128)(4,1)} %bitcast.79), calls=%async_computation.9 | async-start | bytes 6291456
  117.5 5.0 %copy-start.1 = (bf16[1,1,64,7168]{3,2,1,0:T(8,128)(2,1)S(1)}, bf16[1,1,64,7168]{3,2,1,0:T(8,128)(2,1)}, u32[]{:S(2)}) copy-start(bf16[1,1,64,7168]{3,2,1,0:T(8,128)(2,1)} %param.13) | copy-start | bytes 2752516
  117.5 7.3 %copy-start.2 = (s32[64,8]{0,1:T(8,128)S(1)}, s32[64,8]{0,1:T(8,128)}, u32[]{:S(2)}) copy-start(s32[64,8]{0,1:T(8,128)} %param.9) | copy-start | bytes 6148
  117.5 87.8 %all-to-all-start.1 = ((bf16[8,64,7168]{2,1,0:T(8,128)(2,1)}), bf16[8,64,7168]{2,1,0:T(8,128)(2,1)}, u32[]{:S(2)}, u32[]{:S(2)}) async-start(bf16[8,64,7168]{2,1,0:T(8,128)(2,1)} %convolution_convert_fusion), calls=%async_computation.1 | async-start | bytes 14680064 | tf_op jit(solution)/shard_map/all_to_all | solution.py:62
  122.5 110.6 %reduce-scatter.5.cloned.1.call-start = ((), (), s32[]{:S(2)}) async-start(), calls=%async_computation.5 | async-start | bytes 2293760 | tf_op jit(solution)/shard_map/reduce_scatter | solution.py:50
  124.5 133.4 %reduce-scatter.3.cloned.1.call-start = ((), (), s32[]{:S(2)}) async-start(), calls=%async_computation.4 | async-start | bytes 1146880 | tf_op jit(solution)/shard_map/reduce_scatter | solution.py:70
Sparse Core Ops, SparseCore 0:
  125.6 41.1 reduce-scatter.4
  233.2 24.5 reduce-scatter.2
where the time goes:
time: 265 us
  waiting for transfers between devices  102 us (38%)
  blocking collectives  88 us (33%)
  local copies, waits for them, and re-layouts  22.4 us (8%)
  matrix products  21.1 us (8%)
  between operations  14.2 us (5%)
  other arithmetic  11.5 us (4%)
  starting transfers between devices  5.24 us (2%)
    all_to_all x1, blocking collectives, shards(): lax.all_to_all(outgoing, 'expert', split_axis=0, concat_axis=0, tiled=True)  88 us
    all_to_all x1, waiting for transfers between devices, shards(): lax.all_to_all(partial_out.reshape(experts_all, capacity, width), 'expert...  80.3 us
    reduce_scatter x1, waiting for transfers between devices, shards(): lax.psum_scatter(own_sum.astype(jnp.bfloat16), 'dp', scatter_dimension=1,...  21.8 us
    gather x1, local copies, waits for them, and re-layouts, combine_rows(): rows = back.reshape(-1, columns)[places]  17.9 us
    reduce_sum x1, other arithmetic, combine_rows(): return jnp.sum(weighted.reshape(tok_dev, top, columns), axis=1)  9.84 us
    dot_general x1, matrix products, shards(): jnp.einsum('sjcf,jfd->sjcd', hidden, w_down, preferred_element_type=jnp.f...  9.11 us
  transfers between devices with their start and end apart: 3, of which 2 were waited for; matrix products, arithmetic and copies ran while one was open for 12% of the time, Pallas kernels for 0%

commit v1 on v0

v1 whole, which is shorter than its diff:
```python
import functools

import jax
import jax.numpy as jnp
from jax import lax
from jax.experimental import pallas as pl
from jax.experimental.pallas import tpu as pltpu
from jax.sharding import PartitionSpec as P

HESS_COLS = 128


def route_slots(flat_ids, experts_all):
    onehot = (flat_ids[:, None] == jnp.arange(experts_all, dtype=jnp.int32)[None, :]).astype(
        jnp.int32
    )
    earlier = jnp.cumsum(onehot, axis=0) - onehot
    return jnp.sum(earlier * onehot, axis=1)


def combine_rows(back, places, shares, tok_dev, top):
    columns = back.shape[-1]
    rows = back.reshape(-1, columns)[places]
    weighted = rows.astype(jnp.float32) * shares.reshape(-1, 1)
    return jnp.sum(weighted.reshape(tok_dev, top, columns), axis=1)


def route_shares(route_weight):
    weight_counts = route_weight.astype(jnp.float32)
    return 2.5 * weight_counts / jnp.sum(weight_counts, axis=1, keepdims=True)


def gram_window(prev_inputs, n_dp, width):
    history = prev_inputs.reshape(prev_inputs.shape[1], prev_inputs.shape[2], width)
    head_cols = history[:, :, :HESS_COLS]
    gram_scale = 2.0 / (n_dp * history.shape[1])
    return lax.psum_scatter(
        (
            jnp.einsum("jrd,jrh->djh", history, head_cols, preferred_element_type=jnp.float32)
            * gram_scale
        ).astype(jnp.bfloat16),
        "dp",
        scatter_dimension=0,
        tiled=True,
    ).astype(jnp.float32)


def slotted(tokens, routes, route_weight, w_gate, w_up, w_down):
    tok_dev, top = routes.shape
    exp_dev = w_gate.shape[0]
    width = tokens.shape[1]
    n_expert = lax.axis_size("expert")
    experts_all = exp_dev * n_expert
    capacity = min(tok_dev, tok_dev * top * 5 // (4 * experts_all))
    flat_ids = routes.reshape(-1)
    slots = route_slots(flat_ids, experts_all)
    places = flat_ids * capacity + slots
    shares = route_shares(route_weight)
    picks = jnp.arange(experts_all * capacity, dtype=jnp.int32)[:, None] == places[None, :]
    placing = jnp.any(picks.reshape(experts_all * capacity, tok_dev, top), axis=2).astype(
        jnp.bfloat16
    )
    outgoing = jnp.dot(placing, tokens, preferred_element_type=jnp.float32).astype(jnp.bfloat16)
    outgoing = outgoing.reshape(experts_all, capacity, width)
    arrived = lax.all_to_all(outgoing, "expert", split_axis=0, concat_axis=0, tiled=True)
    arrived = arrived.reshape(n_expert, exp_dev, capacity, width)
    gate = jnp.einsum("sjcd,jdf->sjcf", arrived, w_gate, preferred_element_type=jnp.float32)
    up = jnp.einsum("sjcd,jdf->sjcf", arrived, w_up, preferred_element_type=jnp.float32)
    hidden = (jax.nn.silu(gate) * up).astype(jnp.bfloat16)
    partial_out = jnp.einsum("sjcf,jfd->sjcd", hidden, w_down, preferred_element_type=jnp.float32)
    partial_out = partial_out.astype(jnp.bfloat16)
    back = lax.all_to_all(
        partial_out.reshape(experts_all, capacity, width),
        "expert",
        split_axis=0,
        concat_axis=0,
        tiled=True,
    )
    own_sum = combine_rows(back, places, shares, tok_dev, top)
    return lax.psum_scatter(own_sum.astype(jnp.bfloat16), "dp", scatter_dimension=1, tiled=True)

LANES = 128
MESH = pl.DeviceIdType.MESH


def flip(index, bit):
    return index + bit - 2 * bit * ((index // bit) % 2)


def dense_kernel(
    n_dp,
    n_expert,
    tokens,
    share_in,
    w_gate,
    w_up,
    w_down,
    prev,
    mixed_ref,
    hess_ref,
    xall,
    share_all,
    wg,
    wu,
    wd,
    g_acc,
    u_acc,
    hid,
    mine,
    sb0,
    rb0,
    sb1,
    rb1,
    sb2,
    rb2,
    sb3,
    rb3,
    hx,
    hh,
    lsem,
    send_sem,
    recv_sem,
):
    me = lax.axis_index("expert")
    my_dp = lax.axis_index("dp")
    core, xx, yy = me % 2, (me // 2) % 2, (me // 4) % 2
    peer, ex, ey = flip(me, 1), flip(me, 2), flip(me, 4)
    ed = flip(ex, 4)
    chunks, depth = xall.shape[0], xall.shape[-1]
    rows = xall.shape[3]
    half = rows // 2
    cols = rb3.shape[-1]
    hidden_w = wg.shape[-1]
    counter = [0]
    local_counter = [0]

    def local(src, dst):
        copy = pltpu.make_async_copy(src, dst, lsem.at[local_counter[0]])
        local_counter[0] += 1
        copy.start()
        return copy

    def remote(src, dst, where):
        copy = pltpu.make_async_remote_copy(
            src_ref=src,
            dst_ref=dst,
            send_sem=send_sem.at[counter[0]],
            recv_sem=recv_sem.at[counter[0]],
            device_id=where,
            device_id_type=MESH,
        )
        counter[0] += 1
        copy.start()
        sent.append(copy)
        return copy

    sent = []
    token_loads = [
        local(tokens.at[:, c * depth : (c + 1) * depth], xall.at[c, core, me // 2])
        for c in range(chunks)
    ]
    hist_own = local(prev.at[:, pl.ds(pl.multiple_of(my_dp * cols, LANES), cols)], hx.at[0])
    head_own = local(prev.at[:, 0:HESS_COLS], hh.at[0])
    share_own = local(share_in, share_all.at[core, me // 2])
    gate_loads, up_loads = [], []
    for c in range(chunks):
        gate_loads.append(local(w_gate.at[c * depth : (c + 1) * depth, :], wg.at[c]))
        up_loads.append(local(w_up.at[c * depth : (c + 1) * depth, :], wu.at[c]))
    turns = [n_dp // 2] + [d for d in range(1, n_dp) if d != n_dp // 2] + [0]
    down_loads = []
    for i, d in enumerate(turns):
        start = pl.multiple_of(((my_dp + d) % n_dp) * cols, LANES)
        down_loads.append(local(w_down.at[:, pl.ds(start, cols)], wd.at[i]))

    barrier = pltpu.get_barrier_semaphore()
    for d in range(1, n_expert):
        pl.semaphore_signal(
            barrier, inc=1, device_id={"expert": (me + d) % n_expert}, device_id_type=MESH
        )
    for d in range(1, n_dp):
        pl.semaphore_signal(
            barrier, inc=1, device_id={"dp": (my_dp + d) % n_dp}, device_id_type=MESH
        )
    pl.semaphore_wait(barrier, n_expert + n_dp - 2)

    to_peer, to_x, to_y = {"expert": peer}, {"expert": ex}, {"expert": ey}
    flow = {}

    def block(c, who):
        return xall.at[c, who % 2, who // 2]

    def own(c):
        token_loads[c].wait()
        for name, where in (("x", to_x), ("y", to_y), ("p", to_peer)):
            flow[c, name] = remote(block(c, me), block(c, me), where)

    def relay(c):
        flow[c, "x"].wait_recv()
        flow[c, "d0"] = remote(block(c, ex).at[0:half], block(c, ex).at[0:half], to_y)
        flow[c, "px"] = remote(block(c, ex), block(c, ex), to_peer)
        flow[c, "y"].wait_recv()
        flow[c, "d1"] = remote(block(c, ey).at[half:rows], block(c, ey).at[half:rows], to_x)
        flow[c, "py"] = remote(block(c, ey), block(c, ey), to_peer)

    def corner(c):
        flow[c, "d0"].wait_recv()
        flow[c, "p0"] = remote(block(c, ed).at[0:half], block(c, ed).at[0:half], to_peer)
        flow[c, "d1"].wait_recv()
        flow[c, "p1"] = remote(block(c, ed).at[half:rows], block(c, ed).at[half:rows], to_peer)

    tile = 2 * LANES

    def widen(c):
        for name in ("p", "px", "py", "p0", "p1"):
            flow[c, name].wait_recv()
        gate_loads[c].wait()
        up_loads[c].wait()

        @pl.loop(0, hidden_w // tile)
        def _(n):
            at = pl.ds(pl.multiple_of(n * tile, tile), tile)
            x = xall[c].reshape(n_expert * rows, depth)
            g = jnp.dot(x, wg[c, :, at], preferred_element_type=jnp.float32)
            u = jnp.dot(x, wu[c, :, at], preferred_element_type=jnp.float32)
            if c == 0:
                g_acc[:, at] = g
                u_acc[:, at] = u
            else:
                g_acc[:, at] += g
                u_acc[:, at] += u

    own(0)
    share_own.wait()
    share_flows = [
        remote(
            share_all.at[core, me // 2],
            share_all.at[core, me // 2],
            {"expert": (me + d) % n_expert},
        )
        for d in range(1, n_expert)
    ]
    hist_flows = []
    for d in range(1, n_dp):
        start = pl.multiple_of(((my_dp + d) % n_dp) * cols, LANES)
        where = {"dp": (my_dp + d) % n_dp}
        hist_flows.append(remote(prev.at[:, pl.ds(start, cols)], hx.at[d], where))
        hist_flows.append(remote(prev.at[:, 0:HESS_COLS], hh.at[d], where))

    for c in range(chunks + 2):
        if 1 <= c < chunks:
            own(c)
        if 1 <= c <= chunks:
            relay(c - 1)
        if 2 <= c:
            corner(c - 2)
            if c == chunks + 1:
                hist_own.wait()
                head_own.wait()
                for copy in hist_flows:
                    copy.wait_recv()
                scale = 2.0 / (n_dp * hx.shape[1])

                @pl.loop(0, cols // tile)
                def _(n):
                    at = pl.multiple_of(n * tile, tile)
                    left = hx[:, :, pl.ds(at, tile)].reshape(n_dp * hx.shape[1], tile)
                    right = hh[...].reshape(n_dp * hx.shape[1], HESS_COLS)
                    gram = lax.dot_general(
                        left, right, (((0,), (0,)), ((), ())), preferred_element_type=jnp.float32
                    )
                    hess_ref[pl.ds(at, tile), :] = gram * scale

                for copy in share_flows:
                    copy.wait_recv()
            widen(c - 2)

    for kind in range(2):
        span = slice(kind * n_expert // 2 * rows, (kind + 1) * n_expert // 2 * rows)
        sh = share_all[kind].reshape(n_expert // 2 * rows, LANES)
        lane = lax.broadcasted_iota(jnp.int32, sh.shape, 1)
        own_share = jnp.sum(jnp.where(lane == me, sh, 0.0), axis=1, keepdims=True)
        g = g_acc[span, :]
        hid[kind] = (g / (1.0 + jnp.exp(-g)) * u_acc[span, :] * own_share).astype(jnp.bfloat16)

    stage = {}
    chips = n_expert // 2

    def down(i):
        down_loads[i].wait()

        @pl.loop(0, cols // tile)
        def _(n):
            at = pl.ds(pl.multiple_of(n * tile, tile), tile)
            out = jnp.dot(hid[1 - core], wd[i, :, at], preferred_element_type=jnp.float32)
            sb0[i, :, :, at] = out.astype(jnp.bfloat16).reshape(chips, rows, tile)

        stage[i, 0] = remote(sb0.at[i], rb0.at[i], to_peer)

        @pl.loop(0, cols // tile)
        def _(n):
            at = pl.ds(pl.multiple_of(n * tile, tile), tile)
            out = jnp.dot(hid[core], wd[i, :, at], preferred_element_type=jnp.float32)
            mine[i, :, :, at] = out.reshape(chips, rows, tile)

    low, high = slice(0, half), slice(half, rows)

    def both(i, chip, part):
        return mine[i, chip, part, :] + rb0[i, chip, part, :].astype(jnp.float32)

    def first(i):
        stage[i, 0].wait_recv()
        for k in range(2):
            sb1[i, 0, k] = both(i, k * 2 + 1 - xx, low).astype(jnp.bfloat16)
        stage[i, 1] = remote(sb1.at[i, 0], rb1.at[i, 0], to_x)
        for k in range(2):
            sb1[i, 1, k] = both(i, (1 - yy) * 2 + k, high).astype(jnp.bfloat16)
        stage[i, 2] = remote(sb1.at[i, 1], rb1.at[i, 1], to_y)

    def second(i):
        stage[i, 1].wait_recv()
        out = both(i, (1 - yy) * 2 + xx, low) + rb1[i, 0, 1 - yy].astype(jnp.float32)
        sb2[i, 0] = out.astype(jnp.bfloat16)
        stage[i, 3] = remote(sb2.at[i, 0], rb2.at[i, 0], to_y)
        stage[i, 2].wait_recv()
        out = both(i, yy * 2 + 1 - xx, high) + rb1[i, 1, 1 - xx].astype(jnp.float32)
        sb2[i, 1] = out.astype(jnp.bfloat16)
        stage[i, 4] = remote(sb2.at[i, 1], rb2.at[i, 1], to_x)

    def third(i):
        d = turns[i]
        chip = me // 2
        stage[i, 3].wait_recv()
        stage[i, 4].wait_recv()
        top = both(i, chip, low) + rb1[i, 0, yy].astype(jnp.float32)
        top = top + rb2[i, 0].astype(jnp.float32)
        end = both(i, chip, high) + rb1[i, 1, xx].astype(jnp.float32)
        end = end + rb2[i, 1].astype(jnp.float32)
        if d:
            sb3[d - 1, low, :] = top.astype(jnp.bfloat16)
            sb3[d - 1, high, :] = end.astype(jnp.bfloat16)
            stage[i, 5] = remote(
                sb3.at[d - 1], rb3.at[d - 1], {"dp": (my_dp + d) % n_dp}
            )
        else:
            for j, other in enumerate(turns):
                if other:
                    stage[j, 5].wait_recv()
                    top = top + rb3[other - 1, low, :].astype(jnp.float32)
                    end = end + rb3[other - 1, high, :].astype(jnp.float32)
            mixed_ref[low, :] = top.astype(jnp.bfloat16)
            mixed_ref[high, :] = end.astype(jnp.bfloat16)

    for step in range(n_dp + 4):
        if step < n_dp:
            down(step)
        if 1 <= step <= n_dp:
            first(step - 1)
        if 3 <= step < n_dp + 3:
            second(step - 3)
        if 4 <= step:
            third(step - 4)
    for copy in sent:
        copy.wait_send()


def everyone(tokens, routes, route_weight, w_gate, w_up, w_down, prev_inputs):
    rows, width = tokens.shape
    n_expert = lax.axis_size("expert")
    n_dp = lax.axis_size("dp")
    hidden_w = w_gate.shape[2]
    shares = route_shares(route_weight)
    named = routes[:, :, None] == jnp.arange(LANES, dtype=jnp.int32)[None, None, :]
    by_expert = jnp.sum(jnp.where(named, shares[:, :, None], 0.0), axis=1)
    prev = prev_inputs.reshape(prev_inputs.shape[2], width)
    cols = width // n_dp
    chunks = 4
    depth = width // chunks
    chips = n_expert // 2
    total = n_expert * rows
    bf16, f32 = jnp.bfloat16, jnp.float32
    copies = 9 * chunks + (n_expert - 1) + 2 * (n_dp - 1) + 5 * n_dp + n_dp - 1
    vmem = pl.BlockSpec(memory_space=pltpu.VMEM)
    hbm = pl.BlockSpec(memory_space=pl.ANY)
    mixed, hess = pl.pallas_call(
        functools.partial(dense_kernel, n_dp, n_expert),
        out_shape=(
            jax.ShapeDtypeStruct((rows, cols), bf16),
            jax.ShapeDtypeStruct((cols, HESS_COLS), f32),
        ),
        in_specs=[hbm] * 6,
        out_specs=(vmem, vmem),
        scratch_shapes=[
            pltpu.VMEM((chunks, 2, chips, rows, depth), bf16),
            pltpu.VMEM((2, chips, rows, LANES), f32),
            pltpu.VMEM((chunks, depth, hidden_w), bf16),
            pltpu.VMEM((chunks, depth, hidden_w), bf16),
            pltpu.VMEM((n_dp, hidden_w, cols), bf16),
            pltpu.VMEM((total, hidden_w), f32),
            pltpu.VMEM((total, hidden_w), f32),
            pltpu.VMEM((2, total // 2, hidden_w), bf16),
            pltpu.VMEM((n_dp, chips, rows, cols), f32),
            pltpu.VMEM((n_dp, chips, rows, cols), bf16),
            pltpu.VMEM((n_dp, chips, rows, cols), bf16),
            pltpu.VMEM((n_dp, 2, 2, rows // 2, cols), bf16),
            pltpu.VMEM((n_dp, 2, 2, rows // 2, cols), bf16),
            pltpu.VMEM((n_dp, 2, rows // 2, cols), bf16),
            pltpu.VMEM((n_dp, 2, rows // 2, cols), bf16),
            pltpu.VMEM((n_dp - 1, rows, cols), bf16),
            pltpu.VMEM((n_dp - 1, rows, cols), bf16),
            pltpu.VMEM((n_dp, prev.shape[0], cols), bf16),
            pltpu.VMEM((n_dp, prev.shape[0], HESS_COLS), bf16),
            pltpu.SemaphoreType.DMA((3 * chunks + n_dp + 3,)),
            pltpu.SemaphoreType.DMA((copies,)),
            pltpu.SemaphoreType.DMA((copies,)),
        ],
        compiler_params=pltpu.CompilerParams(
            collective_id=0, has_side_effects=True, vmem_limit_bytes=67043328
        ),
        name="dense_layer",
    )(tokens, by_expert, w_gate[0], w_up[0], w_down[0], prev)
    return mixed, hess.reshape(cols, 1, HESS_COLS)


def shards(tokens, routes, route_weight, w_gate, w_up, w_down, prev_inputs):
    n_expert = lax.axis_size("expert")
    if w_gate.shape[0] == 1 and routes.shape[1] == n_expert == 2 * 2 * 2:
        return everyone(tokens, routes, route_weight, w_gate, w_up, w_down, prev_inputs)
    hessian = gram_window(prev_inputs, lax.axis_size("dp"), tokens.shape[1])
    return slotted(tokens, routes, route_weight, w_gate, w_up, w_down), hessian


def solution(mesh):
    placed = (
        P("expert", None),
        P("expert", None),
        P("expert", None),
        P("expert", None, "dp"),
        P("expert", None, "dp"),
        P("expert", "dp", None),
        P("dp", "expert", None, None),
    )
    return jax.shard_map(
        shards,
        mesh=mesh,
        in_specs=placed,
        out_specs=(P("expert", "dp"), P("dp", "expert", None)),
        check_vma=False,
    )
```

time: 265 us -> 103 us (0.39)
  waiting for transfers between devices: 102 us -> 0 us
  Pallas kernels: 0 us -> 95.9 us
  blocking collectives: 88 us -> 0 us
  matrix products: 21.1 us -> 0 us
  local copies, waits for them, and re-layouts: 22.4 us -> 4.47 us
  between operations: 14.2 us -> 0.64 us
  other arithmetic: 11.5 us -> 2.22 us
  starting transfers between devices: 5.24 us -> 0 us
    pallas_call x0 -> x1, Pallas kernels: none -> 95.9 us  [everyone(): pl.pallas_call(functools.partial(dense_kernel, n_dp, n_expert), out_shape...]
    all_to_all x1 -> x0, blocking collectives: 88 us -> none  [shards(): lax.all_to_all(outgoing, 'expert', split_axis=0, concat_axis=0, tiled=True)]
    all_to_all x1 -> x0, waiting for transfers between devices: 80.3 us -> none  [shards(): lax.all_to_all(partial_out.reshape(experts_all, capacity, width), 'expert...]
    reduce_scatter x2 -> x0, waiting for transfers between devices: 21.8 us -> none  [the longest x1 21.8 us: shards(): lax.psum_scatter(own_sum.astype(jnp.bfloat16), 'dp', scatter_dimension=1,...]
    dot_general x5 -> x0, matrix products: 21.1 us -> none  [the longest x1 9.11 us: shards(): jnp.einsum('sjcf,jfd->sjcd', hidden, w_down, preferred_element_type=jnp.f...]
    gather x1 -> x0, local copies, waits for them, and re-layouts: 17.9 us -> none  [combine_rows(): rows = back.reshape(-1, columns)[places]]
    reduce_sum x3 -> x2, other arithmetic: 9.95 us -> 1.53 us  [the longest x1 0.82 us: everyone(): by_expert = jnp.sum(jnp.where(named, shares[:, :, None], 0.0), axis=1)]
    all_to_all x1 -> x0, starting transfers between devices: 4.97 us -> none  [shards(): lax.all_to_all(partial_out.reshape(experts_all, capacity, width), 'expert...]
  transfers between devices with their start and end apart: 3 -> 0, of which waited for: 2 -> 0; matrix products, arithmetic and copies ran while one was open for 12% -> 0% of each run, Pallas kernels for 0% -> 0%
where the time goes in v1:
time: 103 us
  Pallas kernels  95.9 us (93%)
  local copies, waits for them, and re-layouts  4.47 us (4%)
  other arithmetic  2.22 us (2%)
    pallas_call x1, Pallas kernels, everyone(): pl.pallas_call(functools.partial(dense_kernel, n_dp, n_expert), out_shape...  95.9 us
    unnamed x3, local copies, waits for them, and re-layouts  4.38 us

profile of v1, /device:TPU:0, one launch (start us, length us, event | category | flops | bytes accessed | tf_op | source)
XLA Modules:
  0.0 103.2 jit_solution(16164608990135051158)
XLA Ops:
  0.6 0.7 convert_reduce_fusion
  1.3 0.7 multiply_divide_fusion
  2.0 0.1 copy.13
  2.1 0.8 copy.12
  2.9 0.8 select_reduce_fusion.share_in
  3.7 95.9 %dense_layer.1 = (bf16[64,1792]{1,0:T(8,128)(2,1)}, f32[1792,128]{1,0:T(8,128)}) custom-call(bf16[64,7168]{1,0:T(8,128)(2,1)} %tokens.1, f32[64,128]{1,0:T(8,128)} %select_reduce_fusion.share_in, bf16[7168,512]{1,0:T(8,128)(2,1)} %bitcast.7, bf16[7168,512]{1,0:T(8,128)(2,1)} %bitcast.8, bf16[512,7168]{1,0:T(8,128)(2,1)} %bitcast.9, bf16[64,7168]{1,0:T(8,128)(2,1)} %bitcast.11), custom_call_target="tpu_custom_call" | custom-call | tf_op jit(solution)/shard_map/dense_layer/pallas_call | solution.py:384
  99.6 1.6 %copy.17 = bf16[64,1792]{1,0:T(8,128)(2,1)} copy(bf16[64,1792]{1,0:T(8,128)(2,1)} %get-tuple-element.12) | data formatting | bytes 458752
  101.2 2.0 %copy.18 = f32[1792,1,128]{2,1,0:T(1,128)} copy(f32[1792,1,128]{2,1,0:T(1,128)} %bitcast.10) | data formatting | bytes 1835008

commit v2 on v1

--- a/solution.py
+++ b/solution.py
@@ -155,17 +155,22 @@
         return copy
 
     sent = []
+    side = my_dp % 2
+    last = chunks - 1
+
+    def piece(c):
+        return pl.ds(pl.multiple_of((side * last + c * (1 - 2 * side)) * depth, LANES), depth)
+
     token_loads = [
-        local(tokens.at[:, c * depth : (c + 1) * depth], xall.at[c, core, me // 2])
-        for c in range(chunks)
+        local(tokens.at[:, piece(c)], xall.at[c, core, me // 2]) for c in range(chunks)
     ]
     hist_own = local(prev.at[:, pl.ds(pl.multiple_of(my_dp * cols, LANES), cols)], hx.at[0])
     head_own = local(prev.at[:, 0:HESS_COLS], hh.at[0])
     share_own = local(share_in, share_all.at[core, me // 2])
     gate_loads, up_loads = [], []
     for c in range(chunks):
-        gate_loads.append(local(w_gate.at[c * depth : (c + 1) * depth, :], wg.at[c]))
-        up_loads.append(local(w_up.at[c * depth : (c + 1) * depth, :], wu.at[c]))
+        gate_loads.append(local(w_gate.at[piece(c), :], wg.at[c]))
+        up_loads.append(local(w_up.at[piece(c), :], wu.at[c]))
     turns = [n_dp // 2] + [d for d in range(1, n_dp) if d != n_dp // 2] + [0]
     down_loads = []
     for i, d in enumerate(turns):
@@ -183,6 +188,7 @@
         )
     pl.semaphore_wait(barrier, n_expert + n_dp - 2)
 
+    to_z = {"dp": flip(my_dp, 1)}
     to_peer, to_x, to_y = {"expert": peer}, {"expert": ex}, {"expert": ey}
     flow = {}
 
@@ -191,27 +197,44 @@
 
     def own(c):
         token_loads[c].wait()
-        for name, where in (("x", to_x), ("y", to_y), ("p", to_peer)):
+        ways = (("x", to_x), ("y", to_y), ("p", to_peer))
+        for name, where in ways if c < last else ways[2:]:
             flow[c, name] = remote(block(c, me), block(c, me), where)
 
+    def across(who):
+        return remote(block(0, who), block(last, who), to_z)
+
     def relay(c):
+        if c == last:
+            for name, who in (("x", ex), ("y", ey), ("d", ed)):
+                flow["z" + name].wait_recv()
+                flow[c, "p" + name] = remote(block(c, who), block(c, who), to_peer)
+            return
         flow[c, "x"].wait_recv()
         flow[c, "d0"] = remote(block(c, ex).at[0:half], block(c, ex).at[0:half], to_y)
+        if c == 0:
+            flow["zx"] = across(ex)
         flow[c, "px"] = remote(block(c, ex), block(c, ex), to_peer)
         flow[c, "y"].wait_recv()
         flow[c, "d1"] = remote(block(c, ey).at[half:rows], block(c, ey).at[half:rows], to_x)
+        if c == 0:
+            flow["zy"] = across(ey)
         flow[c, "py"] = remote(block(c, ey), block(c, ey), to_peer)
 
     def corner(c):
+        if c == last:
+            return
         flow[c, "d0"].wait_recv()
         flow[c, "p0"] = remote(block(c, ed).at[0:half], block(c, ed).at[0:half], to_peer)
         flow[c, "d1"].wait_recv()
         flow[c, "p1"] = remote(block(c, ed).at[half:rows], block(c, ed).at[half:rows], to_peer)
+        if c == 0:
+            flow["zd"] = across(ed)
 
     tile = 2 * LANES
 
     def widen(c):
-        for name in ("p", "px", "py", "p0", "p1"):
+        for name in ("p", "px", "py", "p0", "p1") if c < last else ("p", "px", "py", "pd"):
             flow[c, name].wait_recv()
         gate_loads[c].wait()
         up_loads[c].wait()
@@ -240,11 +263,13 @@
         for d in range(1, n_expert)
     ]
     hist_flows = []
-    for d in range(1, n_dp):
-        start = pl.multiple_of(((my_dp + d) % n_dp) * cols, LANES)
-        where = {"dp": (my_dp + d) % n_dp}
-        hist_flows.append(remote(prev.at[:, pl.ds(start, cols)], hx.at[d], where))
-        hist_flows.append(remote(prev.at[:, 0:HESS_COLS], hh.at[d], where))
+
+    def send_history():
+        for d in range(1, n_dp):
+            start = pl.multiple_of(((my_dp + d) % n_dp) * cols, LANES)
+            where = {"dp": (my_dp + d) % n_dp}
+            hist_flows.append(remote(prev.at[:, pl.ds(start, cols)], hx.at[d], where))
+            hist_flows.append(remote(prev.at[:, 0:HESS_COLS], hh.at[d], where))
 
     for c in range(chunks + 2):
         if 1 <= c < chunks:
@@ -253,27 +278,12 @@
             relay(c - 1)
         if 2 <= c:
             corner(c - 2)
-            if c == chunks + 1:
-                hist_own.wait()
-                head_own.wait()
-                for copy in hist_flows:
-                    copy.wait_recv()
-                scale = 2.0 / (n_dp * hx.shape[1])
-
-                @pl.loop(0, cols // tile)
-                def _(n):
-                    at = pl.multiple_of(n * tile, tile)
-                    left = hx[:, :, pl.ds(at, tile)].reshape(n_dp * hx.shape[1], tile)
-                    right = hh[...].reshape(n_dp * hx.shape[1], HESS_COLS)
-                    gram = lax.dot_general(
-                        left, right, (((0,), (0,)), ((), ())), preferred_element_type=jnp.float32
-                    )
-                    hess_ref[pl.ds(at, tile), :] = gram * scale
-
-                for copy in share_flows:
-                    copy.wait_recv()
+            if c == 2:
+                send_history()
             widen(c - 2)
 
+    for copy in share_flows:
+        copy.wait_recv()
     for kind in range(2):
         span = slice(kind * n_expert // 2 * rows, (kind + 1) * n_expert // 2 * rows)
         sh = share_all[kind].reshape(n_expert // 2 * rows, LANES)
@@ -296,6 +306,7 @@
 
         stage[i, 0] = remote(sb0.at[i], rb0.at[i], to_peer)
 
+    def keep(i):
         @pl.loop(0, cols // tile)
         def _(n):
             at = pl.ds(pl.multiple_of(n * tile, tile), tile)
@@ -350,11 +361,31 @@
             mixed_ref[low, :] = top.astype(jnp.bfloat16)
             mixed_ref[high, :] = end.astype(jnp.bfloat16)
 
+    def gram():
+        hist_own.wait()
+        head_own.wait()
+        for copy in hist_flows:
+            copy.wait_recv()
+        scale = 2.0 / (n_dp * hx.shape[1])
+
+        @pl.loop(0, cols // tile)
+        def _(n):
+            at = pl.multiple_of(n * tile, tile)
+            left = hx[:, :, pl.ds(at, tile)].reshape(n_dp * hx.shape[1], tile)
+            right = hh[...].reshape(n_dp * hx.shape[1], HESS_COLS)
+            product = lax.dot_general(
+                left, right, (((0,), (0,)), ((), ())), preferred_element_type=jnp.float32
+            )
+            hess_ref[pl.ds(at, tile), :] = product * scale
+
     for step in range(n_dp + 4):
         if step < n_dp:
             down(step)
         if 1 <= step <= n_dp:
+            keep(step - 1)
             first(step - 1)
+        if step == n_dp + 1:
+            gram()
         if 3 <= step < n_dp + 3:
             second(step - 3)
         if 4 <= step:

time: 103 us -> 96.8 us (0.940)
  Pallas kernels: 95.9 us -> 89 us
    pallas_call x1, Pallas kernels: 95.9 us -> 89 us  [everyone(): pl.pallas_call(functools.partial(dense_kernel, n_dp, n_expert), out_shape...]
where the time goes in v2:
time: 96.8 us; the launch traced here: 96.3 us
  Pallas kernels  89 us (92%)
  local copies, waits for them, and re-layouts  4.47 us (5%)
  other arithmetic  2.22 us (2%)
    pallas_call x1, Pallas kernels, everyone(): pl.pallas_call(functools.partial(dense_kernel, n_dp, n_expert), out_shape...  89 us
    unnamed x3, local copies, waits for them, and re-layouts  4.38 us

profile of v2, /device:TPU:0, one launch (start us, length us, event | category | flops | bytes accessed | tf_op | source)
XLA Modules:
  0.0 96.3 jit_solution(10830275046982386166)
XLA Ops:
  0.6 0.7 convert_reduce_fusion
  1.3 0.7 multiply_divide_fusion
  2.0 0.1 copy.13
  2.1 0.8 copy.12
  2.9 0.8 select_reduce_fusion.share_in
  3.7 89.0 %dense_layer.1 = (bf16[64,1792]{1,0:T(8,128)(2,1)}, f32[1792,128]{1,0:T(8,128)}) custom-call(bf16[64,7168]{1,0:T(8,128)(2,1)} %tokens.1, f32[64,128]{1,0:T(8,128)} %select_reduce_fusion.share_in, bf16[7168,512]{1,0:T(8,128)(2,1)} %bitcast.7, bf16[7168,512]{1,0:T(8,128)(2,1)} %bitcast.8, bf16[512,7168]{1,0:T(8,128)(2,1)} %bitcast.9, bf16[64,7168]{1,0:T(8,128)(2,1)} %bitcast.11), custom_call_target="tpu_custom_call" | custom-call | tf_op jit(solution)/shard_map/dense_layer/pallas_call | solution.py:415
  92.7 1.6 %copy.17 = bf16[64,1792]{1,0:T(8,128)(2,1)} copy(bf16[64,1792]{1,0:T(8,128)(2,1)} %get-tuple-element.12) | data formatting | bytes 458752
  94.4 2.0 %copy.18 = f32[1792,1,128]{2,1,0:T(1,128)} copy(f32[1792,1,128]{2,1,0:T(1,128)} %bitcast.10) | data formatting | bytes 1835008
